TPU v7x, 32 devices: a whole 2x2x4 slice. The times are simulated.
32 devices in a mesh: node: 8 (over z, x), rep: 4 (over y, core).
Axes of the slice: x: 2, y: 2, z: 4, core: 2. Of those that a mesh axis runs over, the one named last changes fastest.
Arguments:
- features: bfloat16 [163840, 256], P('node'), may hold values from -6 to 6
- w_in: bfloat16 [256, 256], replicated, may hold values from -0.375 to 0.375
- w_out: bfloat16 [256, 256], replicated, may hold values from -0.375 to 0.375
- pos_src: int32 [8, 4, 8, 2], P('node', 'rep'), may hold values from 0 to 159
- pos_dst: int32 [8, 4, 8, 2], P('node', 'rep'), may hold values from 0 to 159
- counts: int32 [8, 4, 8], P('node', 'rep'), may hold values from 1 to 2, as said below
- neg_blocks: int32 [8, 2], P('node'), may hold values from 0 to 159
- neg_pick: int32 [8, 4, 8, 2], P('node', 'rep'), may hold values from 0 to 15
Outputs:
- pos_scores: float32 [8, 4, 8, 2, 128], P('node', 'rep')
- neg_term: float32 [8, 4, 8, 2, 128], P('node', 'rep')
- loss: float32 [], replicated
Inputs may be any that keep to these rules, and one draw needn't show every extreme that they name: `counts`: each entry is at most 2; in every draw one owner receives 2 live slots from every device.
All inputs are finite; a program needn't handle non-finite values.
Results may differ from a plain program's by a relative error of at most 0.0027.
Values may be sent and summed in bfloat16 or wider, within the bound.
A program may use at most 192 MiB of HBM per device.

v0:
```python
import functools

import jax
import jax.numpy as jnp
from jax import lax
from jax.experimental import pallas as pl
from jax.experimental.pallas import tpu as pltpu
from jax.sharding import PartitionSpec as P

BLK = 128
LOADS = 8


def encode(rows_in, w_in, w_out):
    hidden = jax.nn.silu(jnp.dot(rows_in, w_in, preferred_element_type=jnp.float32)).astype(
        jnp.bfloat16
    )
    return jnp.dot(hidden, w_out, preferred_element_type=jnp.float32).astype(jnp.bfloat16)


def softplus(v):
    return jnp.maximum(v, 0.0) + jnp.log1p(jnp.exp(-jnp.abs(v)))


def partner(me, step, n):
    if n & (n - 1):
        return (me + step) % n
    out, bit = 0, 1
    while bit < n:
        out = out + ((me // bit + step // bit) % 2) * bit
        bit *= 2
    return out


def source_of(me, step, n):
    if n & (n - 1):
        return (me + n - step) % n
    return partner(me, step, n)


def mirror(step, n):
    return n - step if n & (n - 1) else step


def kernel(
    n, reps, slots, offers,
    src_ids, dst_ids, counts, neg_ids, picks, asks, features, w_in, w_out,
    pos_out, neg_out, loss_out,
    feat, heard, heard_s, reply, fetched, source, offer_own, pool, mine_sum, node_sums, rep_mine,
    rep_sums,
    load_sem, ask_send, ask_recv, local_sem, rep_send, rep_recv, off_send, off_recv,
    own_sem, near_send, near_recv, fwd_send, fwd_recv, sum_send, sum_recv, all_send, all_recv,
):
    me = lax.axis_index("node")
    rep = lax.axis_index("rep")
    width = feat.shape[2]
    piece = feat.shape[0] // LOADS
    scale = 1.0 / width**0.5
    lows, highs, quarter = pool.shape[1:4]
    low, high = me % lows, me // lows
    per_block = BLK // quarter

    def to_node(j):
        return {"node": j}

    def to_rep(j):
        return {"rep": j}

    def remote(src, dst, send, recv, where):
        return pltpu.make_async_remote_copy(
            src_ref=src, dst_ref=dst, send_sem=send, recv_sem=recv,
            device_id=where, device_id_type=pl.DeviceIdType.MESH,
        )

    loads = [
        pltpu.make_async_copy(
            features.at[pl.ds(s * piece, piece)], feat.at[pl.ds(s * piece, piece)], load_sem.at[s]
        )
        for s in range(LOADS)
    ]
    for load in loads:
        load.start()

    barrier = pltpu.get_barrier_semaphore()

    @pl.loop(1, n)
    def _(step):
        pl.semaphore_signal(
            barrier, inc=1, device_id=to_node(partner(me, step, n)),
            device_id_type=pl.DeviceIdType.MESH,
        )

    for step in range(1, reps):
        pl.semaphore_signal(
            barrier, inc=1, device_id=to_rep((rep + step) % reps),
            device_id_type=pl.DeviceIdType.MESH,
        )
    pl.semaphore_wait(barrier, n - 1 + reps - 1)

    def ask(step):
        to = partner(me, step, n)
        return remote(asks, heard.at[step], ask_send.at[step], ask_recv.at[step], to_node(to))

    @pl.loop(1, n)
    def _(i):
        ask(n - i).start()

    for load in loads:
        load.wait()

    wi = w_in[...]
    wo = w_out[...]

    def encoded(ids):
        rows = jnp.concatenate([feat[i] for i in ids], axis=0)
        return encode(rows, wi, wo)

    piece_at = pl.multiple_of((rep % per_block) * quarter, quarter)
    offer_own[...] = encode(feat[neg_ids[rep // per_block], pl.ds(piece_at, quarter)], wi, wo)

    own = encoded([dst_ids[c, me] for c in range(slots)])
    reply[0] = own.reshape(slots, BLK, width)

    def offer(step):
        return remote(
            offer_own, pool.at[rep, low, high], off_send.at[step], off_recv.at[step],
            to_node(partner(high, step, highs) * lows + low),
        )

    @pl.loop(1, highs)
    def _(i):
        offer(highs - i).start()

    keep = pltpu.make_async_copy(offer_own, pool.at[rep, low, high], own_sem)
    keep.start()

    @pl.loop(1, n)
    def _(step):
        ask(step).wait()

    down = pltpu.make_async_copy(heard, heard_s, local_sem)
    down.start()
    down.wait()

    def answer(step):
        return remote(
            reply.at[step], fetched.at[step], rep_send.at[step], rep_recv.at[step],
            to_node(partner(me, step, n)),
        )

    @pl.loop(1, n)
    def _(i):
        step = n - i
        reply[step] = encoded(
            [heard_s[mirror(step, n), c, me] for c in range(slots)]
        ).reshape(slots, BLK, width)

        @pl.when(i > 1)
        def _():
            answer(step + 1).start()

    @pl.loop(0, n)
    def _(o):
        source[o] = encoded([src_ids[c, o] for c in range(slots)]).reshape(
            slots, BLK, width
        )

        @pl.when(o == 0)
        def _():
            answer(1).start()

    @pl.loop(1, highs)
    def _(step):
        offer(step).wait()

    keep.wait()
    for step in range(1, lows):
        spot = pool.at[rep, low]
        across = remote(
            spot, spot, near_send, near_recv, to_node(high * lows + (low + step) % lows)
        )
        across.start()
        across.wait()
    forwards = []
    for step in range(1, reps):
        to = (rep + step) % reps
        spot = pool.at[rep]
        forwards.append(remote(spot, spot, fwd_send.at[step - 1], fwd_recv.at[step - 1], to_rep(to)))
    for copy in forwards:
        copy.start()
    for copy in forwards:
        copy.wait()

    contract = (((1,), (1,)), ((), ()))

    def one_negative(o, c):
        pick = picks[c, o]
        home = pick // offers
        first = (pick % offers) * per_block
        cand = jnp.concatenate([pool[first + h, home % lows, home // lows] for h in range(per_block)], axis=0)
        scores = scale * lax.dot_general(
            cand, source[o, c], contract, preferred_element_type=jnp.float32
        )
        term = jnp.sum(softplus(scores), axis=0, keepdims=True) * (1.0 / BLK)
        return jnp.where(c < counts[o], term, 0.0)

    def negatives(o, total):
        rows = [one_negative(o, c) for c in range(slots)]
        neg_out[o] = jnp.concatenate(rows, axis=0)
        return total + functools.reduce(jnp.add, rows)

    total = lax.fori_loop(0, n, negatives, jnp.zeros((1, BLK), jnp.float32))

    diagonal = lax.broadcasted_iota(jnp.int32, (BLK, BLK), 0) == lax.broadcasted_iota(
        jnp.int32, (BLK, BLK), 1
    )

    def positives(held, step, o, total):
        rows = []
        for c in range(slots):
            every = lax.dot_general(
                held[step, c], source[o, c], contract, preferred_element_type=jnp.float32
            )
            raw = scale * jnp.sum(jnp.where(diagonal, every, 0.0), axis=0, keepdims=True)
            live = c < counts[o]
            rows.append(jnp.where(live, raw, 0.0))
            total = total + jnp.where(live, softplus(-raw), 0.0)
        pos_out[o] = jnp.concatenate(rows, axis=0)
        return total

    total = positives(reply, 0, me, total)

    def arrived(i, total):
        step = n - i
        answer(step).wait()
        return positives(fetched, step, source_of(me, step, n), total)

    total = lax.fori_loop(1, n, arrived, total)

    asked = lax.fori_loop(0, n, lambda o, s: s + counts[o], jnp.int32(0))
    mine_sum[0:1] = total
    mine_sum[1:2] = jnp.full((1, BLK), asked.astype(jnp.float32))

    def tell(step):
        return remote(
            mine_sum, node_sums.at[step], sum_send.at[step], sum_recv.at[step],
            to_node(partner(me, step, n)),
        )

    @pl.loop(1, n)
    def _(i):
        tell(n - i).start()

    @pl.loop(1, n)
    def _(step):
        tell(step).wait()

    rep_mine[...] = lax.fori_loop(
        1, n, lambda step, sums: sums + node_sums[step], mine_sum[...]
    )
    tells = [
        remote(
            rep_mine, rep_sums.at[step], all_send.at[step], all_recv.at[step],
            to_rep((rep + step) % reps),
        )
        for step in range(1, reps)
    ]
    for copy in tells:
        copy.start()
    for copy in tells:
        copy.wait()
    sums = rep_mine[...]
    for step in range(1, reps):
        sums = sums + rep_sums[step]
    loss = jnp.sum(sums[0:1], axis=1, keepdims=True) / (BLK * sums[1:2, 0:1])
    loss_out[...] = loss


def shards(n, reps, features, w_in, w_out, pos_src, pos_dst, counts, neg_blocks, neg_pick):
    rows, width = features.shape
    owners = pos_dst.shape[2]
    slots = pos_dst.shape[3]
    offers = neg_blocks.shape[1]
    blocks = rows // BLK
    lows = 1 if n % 2 else 2
    smem = pl.BlockSpec(memory_space=pltpu.SMEM)
    vmem = pl.BlockSpec(memory_space=pltpu.VMEM)
    dma = pltpu.SemaphoreType.DMA
    group = pltpu.VMEM((owners, slots, BLK, width), jnp.bfloat16)

    def by_slot(ids):
        return jnp.swapaxes(ids, 2, 3).reshape(slots, owners)

    call = pl.pallas_call(
        functools.partial(kernel, n, reps, slots, offers),
        out_shape=(
            jax.ShapeDtypeStruct((owners, slots, BLK), jnp.float32),
            jax.ShapeDtypeStruct((owners, slots, BLK), jnp.float32),
            jax.ShapeDtypeStruct((1, 1), jnp.float32),
        ),
        in_specs=[smem] * 5 + [vmem, pl.BlockSpec(memory_space=pl.ANY), vmem, vmem],
        out_specs=(vmem, vmem, vmem),
        scratch_shapes=[
            pltpu.VMEM((blocks, BLK, width), jnp.bfloat16),
            pltpu.VMEM((n, slots, owners), jnp.int32),
            pltpu.SMEM((n, slots, owners), jnp.int32),
            group,
            group,
            group,
            pltpu.VMEM((offers * BLK // reps, width), jnp.bfloat16),
            pltpu.VMEM((reps, lows, n // lows, offers * BLK // reps, width), jnp.bfloat16),
            pltpu.VMEM((2, BLK), jnp.float32),
            pltpu.VMEM((n, 2, BLK), jnp.float32),
            pltpu.VMEM((2, BLK), jnp.float32),
            pltpu.VMEM((reps, 2, BLK), jnp.float32),
            dma((LOADS,)),
            dma((n,)),
            dma((n,)),
            dma,
            dma((n,)),
            dma((n,)),
            dma((n,)),
            dma((n,)),
            dma,
            dma,
            dma,
            dma((reps,)),
            dma((reps,)),
            dma((n,)),
            dma((n,)),
            dma((reps,)),
            dma((reps,)),
        ],
        compiler_params=pltpu.CompilerParams(
            collective_id=0, has_side_effects=True, vmem_limit_bytes=67043328
        ),
    )
    pos, neg, loss = call(
        by_slot(pos_src),
        by_slot(pos_dst),
        counts.reshape(-1),
        neg_blocks.reshape(-1),
        by_slot(neg_pick),
        by_slot(pos_dst),
        features.reshape(blocks, BLK, width),
        w_in,
        w_out,
    )
    shape = (1, 1, owners, slots, BLK)
    return pos.reshape(shape), neg.reshape(shape), loss.reshape(())


def solution(mesh):
    return jax.shard_map(
        functools.partial(shards, mesh.shape["node"], mesh.shape["rep"]),
        mesh=mesh,
        in_specs=(
            P("node", None),
            P(),
            P(),
            P("node", "rep", None, None),
            P("node", "rep", None, None),
            P("node", "rep", None),
            P("node", None),
            P("node", "rep", None, None),
        ),
        out_specs=(P("node", "rep", None, None, None), P("node", "rep", None, None, None), P()),
        check_vma=False,
    )
```

profile of v0, /device:TPU:0, one launch (start us, length us, event | category | flops | bytes accessed | tf_op | source)
XLA Modules:
  0.0 53.1 jit_solution(15813351079653153227)
XLA Ops:
  0.6 48.1 %shard_map.103 = (f32[8,2,128]{2,1,0:T(2,128)}, f32[8,2,128]{2,1,0:T(2,128)}, f32[1,1]{1,0:T(1,128)}) custom-call(s32[2,8]{1,0:T(2,128)} %bitcast.20, s32[2,8]{1,0:T(2,128)} %bitcast.18, s32[8]{0:T(128)} %bitcast.22, s32[2]{0:T(128)} %bitcast.23, s32[2,8]{1,0:T(2,128)} %bitcast.21, s32[2,8]{1,0:T(2,128)} %bitcast.19, bf16[160,128,256]{2,1,0:T(8,128)(2,1)} %bitcast.15, ...), custom_call_target="tpu_custom_call" | custom-call | tf_op jit(solution)/shard_map/pallas_call | solution.py:338
  48.8 1.3 %copy.14 = f32[1,1,8,2,128]{4,3,2,1,0:T(2,128)} copy(f32[1,1,8,2,128]{4,3,2,1,0:T(2,128)} %bitcast.17) | data formatting | bytes 16384
  50.1 1.3 %copy.15 = f32[1,1,8,2,128]{4,3,2,1,0:T(2,128)} copy(f32[1,1,8,2,128]{4,3,2,1,0:T(2,128)} %bitcast.16) | data formatting | bytes 16384
where the time goes:
time: 53.4 us; the launch traced here: 53.1 us
  Pallas kernels  48.1 us (90%)
  local copies, waits for them, and re-layouts  2.59 us (5%)
  between operations  2.4 us (4%)
    pallas_call x1, Pallas kernels, shards(): call(by_slot(pos_src), by_slot(pos_dst), counts.reshape(-1), neg_blocks.r...  48.1 us
    unnamed x2, local copies, waits for them, and re-layouts  2.59 us

commit v1 on v0

v1 whole, which is shorter than its diff:
```python
import functools

import jax
import jax.numpy as jnp
from jax import lax
from jax.experimental import pallas as pl
from jax.experimental.pallas import tpu as pltpu
from jax.sharding import PartitionSpec as P

BLK = 128
LOADS = 8
EARLY = 2
UNROLL = 16
SPARE = 6 * 2**20


def encode(rows_in, w_in, w_out):
    hidden = jax.nn.silu(jnp.dot(rows_in, w_in, preferred_element_type=jnp.float32)).astype(
        jnp.bfloat16
    )
    return jnp.dot(hidden, w_out, preferred_element_type=jnp.float32).astype(jnp.bfloat16)


def softplus(v):
    return jnp.maximum(v, 0.0) + jnp.log1p(jnp.exp(-jnp.abs(v)))


def partner(me, step, n):
    if n & (n - 1):
        return (me + step) % n
    out, bit = 0, 1
    while bit < n:
        out = out + ((me // bit + step // bit) % 2) * bit
        bit *= 2
    return out


def source_of(me, step, n):
    if n & (n - 1):
        return (me + n - step) % n
    return partner(me, step, n)


def order(k, n):
    if n & (n - 1) or not 4 <= n <= UNROLL or k >= n // 2:
        return n - 1 - k
    return n // 2 + 2 * (k % (n // 4)) + k // (n // 4)


def in_order(first, last, n, body, carry):
    if n > UNROLL:
        return lax.fori_loop(first, last, lambda k, c: body(n - 1 - k, c), carry)
    for k in range(first, last):
        carry = body(order(k, n), carry)
    return carry


def messages(reps):
    bits = [1 << b for b in reversed(range(reps.bit_length() - 1))]
    return [(bit, held) for bit in bits for held in range(0, reps, 2 * bit)]


def kernel(
    n, reps, slots, offers,
    src_ids, dst_ids, counts, neg_ids, picks, features, w_in, w_out,
    out,
    feat, wi_v, wo_v, asks_in, counts_in, asks, heard,
    src_s, dst_s, counts_s, neg_s, picks_s, heard_s,
    source, target, fetched, back, pool, sums,
    load_sem, weight_sem, id_sem, local_sem,
    ask_send, ask_recv, src_send, src_recv, ret_send, ret_recv,
    far_send, far_recv, near_send, near_recv, hand_send, hand_recv,
    rep_send, rep_recv, all_send, all_recv,
):
    me = lax.axis_index("node")
    rep = lax.axis_index("rep")
    blocks = feat.shape[0]
    owners = src_ids.shape[1]
    width = feat.shape[2]
    piece = blocks // LOADS
    quarter = pool.shape[2]
    per_block = BLK // quarter
    scale = 1.0 / width**0.5
    part = n // 2
    base = (me // part) * part
    far = (me + part) % n

    def to_node(j):
        return {"node": j}

    def to_rep(j):
        return {"rep": j}

    def remote(src, dst, send, recv, where):
        return pltpu.make_async_remote_copy(
            src_ref=src, dst_ref=dst, send_sem=send, recv_sem=recv,
            device_id=where, device_id_type=pl.DeviceIdType.MESH,
        )

    barrier = pltpu.get_barrier_semaphore()

    @pl.loop(1, n)
    def _(i):
        pl.semaphore_signal(
            barrier, inc=1, device_id=to_node(partner(me, n - i, n)),
            device_id_type=pl.DeviceIdType.MESH,
        )

    for step in range(1, reps):
        pl.semaphore_signal(
            barrier, inc=1, device_id=to_rep(partner(rep, step, reps)),
            device_id_type=pl.DeviceIdType.MESH,
        )

    weights = [
        pltpu.make_async_copy(w_in, wi_v, weight_sem.at[0]),
        pltpu.make_async_copy(w_out, wo_v, weight_sem.at[1]),
    ]
    ids = [
        pltpu.make_async_copy(src, dst, id_sem.at[i])
        for i, (src, dst) in enumerate(
            [
                (dst_ids, asks_in), (counts, counts_in), (neg_ids, neg_s), (src_ids, src_s),
                (dst_ids, dst_s), (counts, counts_s), (picks, picks_s),
            ]
        )
    ]
    loads = [
        pltpu.make_async_copy(
            features.at[pl.ds(s * piece, piece)], feat.at[pl.ds(s * piece, piece)], load_sem.at[s]
        )
        for s in range(LOADS)
    ]
    for copy in ids + weights + loads:
        copy.start()
    for copy in ids:
        copy.wait()

    slot = lax.broadcasted_iota(jnp.int32, (slots, owners), 0)
    asks[...] = jnp.where(slot < counts_in[...], asks_in[...], asks_in[...] + blocks)

    for copy in weights + loads:
        copy.wait()

    def encoded(at):
        rows = jnp.concatenate([feat[i] for i in at], axis=0)
        return encode(rows, wi_v[...], wo_v[...]).reshape(slots, BLK, width)

    def encode_source(step):
        o = partner(me, step, n)
        source[step] = encoded([src_s[c, o] for c in range(slots)])

    def send(step):
        return remote(
            source.at[step], fetched.at[step], src_send.at[step], src_recv.at[step],
            to_node(partner(me, step, n)),
        )

    def ask(step):
        return remote(
            asks, heard.at[step], ask_send.at[step], ask_recv.at[step],
            to_node(partner(me, step, n)),
        )

    def near(t, spot, send_sem, recv_sem):
        spot = pool.at[rep, spot]
        peer = base + partner(me % part, t, part)
        return remote(spot, spot, send_sem.at[t], recv_sem.at[t], to_node(peer))

    piece_at = pl.multiple_of((rep % per_block) * quarter, quarter)
    pool[rep, me] = encode(
        feat[neg_s[0, rep // per_block], pl.ds(piece_at, quarter)], wi_v[...], wo_v[...]
    )
    encode_source(order(0, n))
    pl.semaphore_wait(barrier, n - 1 + reps - 1)

    across = remote(pool.at[rep, me], pool.at[rep, me], far_send, far_recv, to_node(far))
    across.start()

    @pl.loop(1, part)
    def _(t):
        near(t, me, near_send, near_recv).start()

    @pl.loop(1, n)
    def _(i):
        ask(n - i).start()

    early = min(EARLY, n - 1)
    for k in range(1, early + 1):
        encode_source(order(k, n))
        send(order(k - 1, n)).start()

    def prepare(step, carry):
        encode_source(step)
        return carry

    in_order(early + 1, n, n, prepare, 0)
    across.wait()

    @pl.loop(1, part)
    def _(t):
        near(t, far, hand_send, hand_recv).start()

    @pl.loop(1, part)
    def _(t):
        near(t, me, near_send, near_recv).wait()

    plan = messages(reps)

    def share(h, i):
        bit, held = plan[i]
        start = (base + h * part) % n
        spot = pool.at[partner(rep, held, reps), pl.ds(start, part)]
        at = h * len(plan) + i
        return remote(
            spot, spot, rep_send.at[at], rep_recv.at[at], to_rep(partner(rep, bit, reps))
        )

    own = [i for i, (_, held) in enumerate(plan) if held == 0]
    passed = [i for i in range(len(plan)) if i not in own]
    for i in own:
        share(0, i).start()

    def release(step, carry):
        send(step).start()
        return carry

    in_order(early, n - 1, n, release, 0)

    @pl.loop(1, n)
    def _(step):
        ask(step).wait()

    down = pltpu.make_async_copy(heard, heard_s, local_sem)
    down.start()
    down.wait()

    def asked(step, c):
        code = heard_s[step, c, me]
        return jnp.where(code < blocks, code, code - blocks), code < blocks

    target[0] = encoded([dst_s[c, me] for c in range(slots)])

    @pl.loop(1, n)
    def _(step):
        target[step] = encoded([asked(step, c)[0] for c in range(slots)])

    @pl.loop(1, part)
    def _(t):
        near(t, far, hand_send, hand_recv).wait()

    for i in own:
        share(1, i).start()
    waited = set()
    for i in passed:
        bit, held = plan[i]
        low = held & -held
        first = plan.index((low, held - low))
        for h in range(2):
            if (h, first) not in waited:
                share(h, first).wait()
                waited.add((h, first))
            share(h, i).start()
    for i in range(len(plan)):
        for h in range(2):
            if (h, i) not in waited:
                share(h, i).wait()

    contract = (((1,), (1,)), ((), ()))

    def one_negative(step, o, c):
        pick = picks_s[c, o]
        home = pick // offers
        first = (pick % offers) * per_block
        cand = jnp.concatenate([pool[first + h, home] for h in range(per_block)], axis=0)
        scores = scale * lax.dot_general(
            cand, source[step, c], contract, preferred_element_type=jnp.float32
        )
        term = jnp.sum(softplus(scores), axis=0, keepdims=True) * (1.0 / BLK)
        return jnp.where(c < counts_s[0, o], term, 0.0)

    def negatives(step, total):
        o = partner(me, step, n)
        rows = [one_negative(step, o, c) for c in range(slots)]
        out[owners + o] = jnp.concatenate(rows, axis=0)
        return total + functools.reduce(jnp.add, rows)

    total = lax.fori_loop(0, n, negatives, jnp.zeros((1, BLK), jnp.float32))

    diagonal = lax.broadcasted_iota(jnp.int32, (BLK, BLK), 0) == lax.broadcasted_iota(
        jnp.int32, (BLK, BLK), 1
    )

    def positives(held, step, live, total):
        rows = []
        for c in range(slots):
            every = lax.dot_general(
                target[step, c], held[step, c], contract, preferred_element_type=jnp.float32
            )
            raw = scale * jnp.sum(jnp.where(diagonal, every, 0.0), axis=0, keepdims=True)
            rows.append(jnp.where(live[c], raw, 0.0))
            total = total + jnp.where(live[c], softplus(-raw), 0.0)
        return jnp.concatenate(rows, axis=0), total

    rows, total = positives(source, 0, [c < counts_s[0, me] for c in range(slots)], total)
    out[me] = rows

    def give(step):
        return remote(
            back.at[step], out.at[me], ret_send.at[step], ret_recv.at[step],
            to_node(source_of(me, step, n)),
        )

    def arrived(step, total):
        send(step).wait()
        rows, total = positives(fetched, step, [asked(step, c)[1] for c in range(slots)], total)
        back[step] = rows
        give(step).start()
        return total

    total = in_order(0, n - 1, n, arrived, total)

    live_slots = lax.fori_loop(0, owners, lambda o, s: s + counts_s[0, o], jnp.int32(0))
    sums[0, 0:1] = total
    sums[0, 1:2] = jnp.full((1, BLK), live_slots.astype(jnp.float32))

    def tell(dn, dr):
        at = dn * reps + dr
        return remote(
            sums.at[0], sums.at[at], all_send.at[at], all_recv.at[at],
            {"node": partner(me, dn, n), "rep": partner(rep, dr, reps)},
        )

    @pl.loop(0, n)
    def _(i):
        for dr in reversed(range(reps)):
            if dr:
                tell(n - 1 - i, dr).start()
            else:

                @pl.when(i < n - 1)
                def _():
                    tell(n - 1 - i, 0).start()

    @pl.loop(1, n)
    def _(step):
        give(step).wait()

    @pl.loop(0, n)
    def _(dn):
        for dr in range(reps):
            if dr:
                tell(dn, dr).wait()
            else:

                @pl.when(dn > 0)
                def _():
                    tell(dn, 0).wait()

    both = jnp.sum(sums[...], axis=0)
    loss = jnp.sum(both[0:1], axis=1, keepdims=True) / (BLK * both[1:2, 0:1])
    out[2 * owners] = jnp.broadcast_to(loss, (slots, BLK))


def split(owners, joined, pos_out, neg_out, loss_out):
    pos_out[...] = joined[0:owners]
    neg_out[...] = joined[owners : 2 * owners]
    loss_out[...] = joined[2 * owners, 0:1, 0:1]


def shards(n, reps, features, w_in, w_out, pos_src, pos_dst, counts, neg_blocks, neg_pick):
    rows, width = features.shape
    owners = pos_dst.shape[2]
    slots = pos_dst.shape[3]
    offers = neg_blocks.shape[1]
    blocks = rows // BLK
    hbm = pl.BlockSpec(memory_space=pltpu.HBM)
    vmem = pl.BlockSpec(memory_space=pltpu.VMEM)
    dma = pltpu.SemaphoreType.DMA
    group = pltpu.VMEM((n, slots, BLK, width), jnp.bfloat16)
    shared = 2 * len(messages(reps))
    held = features.size + 3 * n * slots * BLK * width + n * offers * BLK * width

    def by_slot(ids):
        return jnp.swapaxes(ids, 2, 3).reshape(slots, owners)

    joined = pl.pallas_call(
        functools.partial(kernel, n, reps, slots, offers),
        out_shape=pltpu.VMEM((2 * owners + 1, slots, BLK), jnp.float32),
        in_specs=[hbm] * 8,
        out_specs=vmem,
        scratch_shapes=[
            pltpu.VMEM((blocks, BLK, width), jnp.bfloat16),
            pltpu.VMEM(w_in.shape, jnp.bfloat16),
            pltpu.VMEM(w_out.shape, jnp.bfloat16),
            pltpu.VMEM((slots, owners), jnp.int32),
            pltpu.VMEM((1, owners), jnp.int32),
            pltpu.VMEM((slots, owners), jnp.int32),
            pltpu.VMEM((n, slots, owners), jnp.int32),
            pltpu.SMEM((slots, owners), jnp.int32),
            pltpu.SMEM((slots, owners), jnp.int32),
            pltpu.SMEM((1, owners), jnp.int32),
            pltpu.SMEM((1, offers), jnp.int32),
            pltpu.SMEM((slots, owners), jnp.int32),
            pltpu.SMEM((n, slots, owners), jnp.int32),
            group,
            group,
            group,
            pltpu.VMEM((n, slots, BLK), jnp.float32),
            pltpu.VMEM((reps, n, offers * BLK // reps, width), jnp.bfloat16),
            pltpu.VMEM((n * reps, 2, BLK), jnp.float32),
            dma((LOADS,)),
            dma((2,)),
            dma((7,)),
            dma,
            dma((n,)),
            dma((n,)),
            dma((n,)),
            dma((n,)),
            dma((n,)),
            dma((n,)),
            dma,
            dma,
            dma((n // 2,)),
            dma((n // 2,)),
            dma((n // 2,)),
            dma((n // 2,)),
            dma((max(shared, 1),)),
            dma((max(shared, 1),)),
            dma((n * reps,)),
            dma((n * reps,)),
        ],
        compiler_params=pltpu.CompilerParams(
            collective_id=0, has_side_effects=True, vmem_limit_bytes=2 * held + SPARE
        ),
    )(
        *(
            pltpu.with_memory_space_constraint(array, pltpu.HBM)
            for array in (
                by_slot(pos_src),
                by_slot(pos_dst),
                counts.reshape(1, owners),
                neg_blocks.reshape(1, offers),
                by_slot(neg_pick),
                features.reshape(blocks, BLK, width),
                w_in,
                w_out,
            )
        )
    )
    scores = jax.ShapeDtypeStruct((owners, slots, BLK), jnp.float32)
    pos, neg, loss = pl.pallas_call(
        functools.partial(split, owners),
        out_shape=(scores, scores, jax.ShapeDtypeStruct((1, 1), jnp.float32)),
        in_specs=[vmem],
        out_specs=(vmem, vmem, vmem),
        compiler_params=pltpu.CompilerParams(vmem_limit_bytes=4 * 2**20),
    )(joined)
    shape = (1, 1, owners, slots, BLK)
    return pos.reshape(shape), neg.reshape(shape), loss.reshape(())


def solution(mesh):
    return jax.shard_map(
        functools.partial(shards, mesh.shape["node"], mesh.shape["rep"]),
        mesh=mesh,
        in_specs=(
            P("node", None),
            P(),
            P(),
            P("node", "rep", None, None),
            P("node", "rep", None, None),
            P("node", "rep", None),
            P("node", None),
            P("node", "rep", None, None),
        ),
        out_specs=(P("node", "rep", None, None, None), P("node", "rep", None, None, None), P()),
        check_vma=False,
    )
```

time: 53.4 us -> 42.4 us (0.79)
  Pallas kernels: 48.1 us -> 41.6 us
  local copies, waits for them, and re-layouts: 2.59 us -> 0 us
  between operations: 2.4 us -> 0.64 us
    pallas_call x1 -> x2, Pallas kernels: 48.1 us -> 41.6 us  [the longest x1 41 us: shards(): pl.pallas_call(functools.partial(kernel, n, reps, slots, offers), out_sha...]
    unnamed x2 -> x0, local copies, waits for them, and re-layouts: 2.59 us -> none
where the time goes in v1:
time: 42.4 us; the launch traced here: 42.3 us
  Pallas kernels  41.6 us (98%)
  between operations  0.64 us (2%)
    pallas_call x1, Pallas kernels, shards(): pl.pallas_call(functools.partial(kernel, n, reps, slots, offers), out_sha...  41 us

profile of v1, /device:TPU:0, one launch (start us, length us, event | category | flops | bytes accessed | tf_op | source)
XLA Modules:
  0.0 42.3 jit_solution(2342562599187304614)
XLA Ops:
  0.6 41.0 %shard_map.103.joined = f32[17,2,128]{2,1,0:T(2,128)S(1)} custom-call(s32[2,8]{1,0:T(2,128)} %bitcast.15, s32[2,8]{1,0:T(2,128)} %bitcast.16, s32[1,8]{1,0:T(1,128)} %bitcast.18, s32[1,2]{1,0:T(1,128)} %neg_ids.1, s32[2,8]{1,0:T(2,128)} %bitcast.17, bf16[160,128,256]{2,1,0:T(8,128)(2,1)} %bitcast.14, bf16[256,256]{1,0:T(8,128)(2,1)} %w_in.1, ...), custom_call_target="tpu_custom_call" | custom-call | tf_op jit(solution)/shard_map/pallas_call | solution.py:387
  41.7 0.6 %shard_map.104 = (f32[8,2,128]{2,1,0:T(2,128)}, f32[8,2,128]{2,1,0:T(2,128)}, f32[1,1]{1,0:T(1,128)}) custom-call(f32[17,2,128]{2,1,0:T(2,128)S(1)} %shard_map.103.joined), custom_call_target="tpu_custom_call" | custom-call | tf_op jit(solution)/shard_map/pallas_call | solution.py:452

commit v2 on v1

v2 whole, which is shorter than its diff:
```python
import functools

import jax
import jax.numpy as jnp
from jax import lax
from jax.experimental import pallas as pl
from jax.experimental.pallas import tpu as pltpu
from jax.sharding import PartitionSpec as P

BLK = 128
HALVES = 2
EARLY = 2
UNROLL = 16
SPARE = 6 * 2**20


def encode(rows_in, w_in, w_out):
    hidden = jax.nn.silu(jnp.dot(rows_in, w_in, preferred_element_type=jnp.float32)).astype(
        jnp.bfloat16
    )
    return jnp.dot(hidden, w_out, preferred_element_type=jnp.float32).astype(jnp.bfloat16)


def softplus(v):
    return jnp.maximum(v, 0.0) + jnp.log1p(jnp.exp(-jnp.abs(v)))


def partner(me, step, n):
    if n & (n - 1):
        return (me + step) % n
    out, bit = 0, 1
    while bit < n:
        out = out + ((me // bit + step // bit) % 2) * bit
        bit *= 2
    return out


def source_of(me, step, n):
    if n & (n - 1):
        return (me + n - step) % n
    return partner(me, step, n)


def sequence(n):
    down = list(range(n - 1, 0, -1))
    if n & (n - 1) or n < 4:
        return down
    far = [n // 2 + 2 * (k % (n // 4)) + k // (n // 4) for k in range(n // 2)]
    return far + down[n // 2 :]


def in_order(steps, body, carry):
    if len(steps) < UNROLL:
        for step in steps:
            carry = body(step, carry)
        return carry
    first, last = steps[0], steps[-1]
    return lax.fori_loop(0, first - last + 1, lambda k, c: body(first - k, c), carry)


def messages(reps):
    bits = [1 << b for b in reversed(range(reps.bit_length() - 1))]
    return [(bit, held) for bit in bits for held in range(0, reps, 2 * bit)]


def kernel(
    n, reps, slots, offers,
    src_ids, dst_ids, counts, neg_ids, picks, features, w_in, w_out,
    out,
    feat_a, feat_b, wi_v, wo_v, asks_in, counts_in, asks, heard,
    id_s, counts_s, neg_s, heard_s,
    source, target, fetched, back, pool, sums,
    load_sem, weight_sem, id_sem, local_sem,
    ask_send, ask_recv, src_send, src_recv, ret_send, ret_recv,
    far_send, far_recv, near_send, near_recv, hand_send, hand_recv,
    rep_send, rep_recv, rest_recv, all_send, all_recv,
):
    me = lax.axis_index("node")
    rep = lax.axis_index("rep")
    blocks, rows, width = feat_a.shape
    owners = src_ids.shape[1]
    src_s, dst_s, picks_s = (id_s.at[i] for i in range(3))
    quarter = pool.shape[2]
    per_block = BLK // quarter
    scale = 1.0 / width**0.5
    part = n // 2
    base = (me // part) * part
    far = (me + part) % n
    steps = sequence(n) if n <= UNROLL else list(range(n - 1, 0, -1))
    piece_at = (rep % per_block) * quarter
    first_half = piece_at // rows

    def to_node(j):
        return {"node": j}

    def to_rep(j):
        return {"rep": j}

    def remote(src, dst, send, recv, where):
        return pltpu.make_async_remote_copy(
            src_ref=src, dst_ref=dst, send_sem=send, recv_sem=recv,
            device_id=where, device_id_type=pl.DeviceIdType.MESH,
        )

    barrier = pltpu.get_barrier_semaphore()

    @pl.loop(1, n)
    def _(i):
        pl.semaphore_signal(
            barrier, inc=1, device_id=to_node(partner(me, n - i, n)),
            device_id_type=pl.DeviceIdType.MESH,
        )

    for step in range(1, reps):
        pl.semaphore_signal(
            barrier, inc=1, device_id=to_rep(partner(rep, step, reps)),
            device_id_type=pl.DeviceIdType.MESH,
        )

    weights = [
        pltpu.make_async_copy(w_in, wi_v, weight_sem.at[0]),
        pltpu.make_async_copy(w_out, wo_v, weight_sem.at[1]),
    ]
    ids = [
        pltpu.make_async_copy(src_ids, src_s, id_sem.at[0]),
        pltpu.make_async_copy(dst_ids, dst_s, id_sem.at[0]),
        pltpu.make_async_copy(picks, picks_s, id_sem.at[0]),
        pltpu.make_async_copy(counts, counts_s, id_sem.at[1]),
        pltpu.make_async_copy(neg_ids, neg_s, id_sem.at[2]),
        pltpu.make_async_copy(dst_ids, asks_in, id_sem.at[3]),
        pltpu.make_async_copy(counts, counts_in, id_sem.at[4]),
    ]
    loads = [
        pltpu.make_async_copy(
            features.at[pl.ds(0, blocks), (first_half + j) % HALVES], buffer, load_sem.at[j]
        )
        for j, buffer in enumerate((feat_a, feat_b))
    ]
    for copy in ids + weights + loads:
        copy.start()
    pltpu.make_async_copy(id_s, id_s, id_sem.at[0]).wait()
    for copy in ids[3:]:
        copy.wait()

    slot = lax.broadcasted_iota(jnp.int32, (slots, owners), 0)
    asks[...] = jnp.where(slot < counts_in[...], asks_in[...], asks_in[...] + blocks)

    for copy in weights + loads[:1]:
        copy.wait()

    def run(parts):
        return encode(jnp.concatenate(parts, axis=0), wi_v[...], wo_v[...])

    def encoded(held, at, ids):
        both = run([buffer[i] for buffer in (feat_a, feat_b) for i in ids])
        both = both.reshape(HALVES, slots, rows, width)
        for j in range(HALVES):
            held[at, (first_half + j) % HALVES] = both[j]

    def source_ids(step):
        o = partner(me, step, n)
        return [src_s[c, o] for c in range(slots)]

    def encode_source(step):
        encoded(source, step, source_ids(step))

    def send(step):
        return remote(
            source.at[step], fetched.at[step], src_send, src_recv.at[step - 1],
            to_node(partner(me, step, n)),
        )

    def encode_half(step, j, buffer):
        half = run([buffer[i] for i in source_ids(step)])
        source[step, (first_half + j) % HALVES] = half.reshape(slots, rows, width)

    def send_half(step, j):
        h = (first_half + j) % HALVES
        return remote(
            source.at[step, h], fetched.at[step, h], src_send, src_recv.at[step - 1],
            to_node(partner(me, step, n)),
        )

    def block(held, at, c):
        return jnp.concatenate([held[at, h, c] for h in range(HALVES)], axis=0)

    def ask(step):
        return remote(
            asks, heard.at[step], ask_send, ask_recv,
            to_node(partner(me, step, n)),
        )

    def near(t, spot, send_sem, recv_sem):
        spot = pool.at[rep, spot]
        peer = base + partner(me % part, t, part)
        return remote(spot, spot, send_sem, recv_sem, to_node(peer))

    def all_near(send_sem, recv_sem):
        spot = pool.at[rep, pl.ds(0, part - 1)]
        return remote(spot, spot, send_sem, recv_sem, to_node(far))

    piece = pl.ds(pl.multiple_of(piece_at % rows, quarter), quarter)
    pool[rep, me] = run([feat_a[neg_s[0, rep // per_block], piece]])
    encode_half(steps[0], 0, feat_a)
    pl.semaphore_wait(barrier, n - 1 + reps - 1)

    across = remote(pool.at[rep, me], pool.at[rep, me], far_send, far_recv, to_node(far))
    across.start()

    @pl.loop(1, part)
    def _(t):
        near(t, me, near_send, near_recv).start()

    @pl.loop(1, n)
    def _(i):
        ask(n - i).start()

    send_half(steps[0], 0).start()
    loads[1].wait()
    encode_half(steps[0], 1, feat_b)
    for before, step in zip(steps[:EARLY], steps[1 : EARLY + 1]):
        encode_source(step)
        (send_half(before, 1) if before == steps[0] else send(before)).start()

    def prepare(step, carry):
        encode_source(step)
        return carry

    in_order(steps[EARLY + 1 :], prepare, 0)
    encode_source(0)

    across.wait()

    @pl.loop(1, part)
    def _(t):
        near(t, far, hand_send, hand_recv).start()

    all_near(near_send, near_recv).wait()

    plan = messages(reps)
    parents = [i for i, (bit, _) in enumerate(plan) if bit > 1]

    def share(h, i):
        bit, held = plan[i]
        start = (base + h * part) % n
        spot = pool.at[partner(rep, held, reps), pl.ds(start, part)]
        got = rep_recv.at[parents.index(i) * 2 + h] if i in parents else rest_recv
        return remote(spot, spot, rep_send, got, to_rep(partner(rep, bit, reps)))

    own = [i for i, (_, held) in enumerate(plan) if held == 0]
    passed = [i for i in range(len(plan)) if i not in own]
    for i in own:
        share(0, i).start()

    def release(step, carry):
        send(step).start()
        return carry

    in_order(steps[EARLY:], release, 0)

    got = heard.at[pl.ds(1, n - 1)]
    remote(got, got, ask_send, ask_recv, to_node(far)).wait()

    down = pltpu.make_async_copy(heard, heard_s, local_sem)
    down.start()
    down.wait()

    def asked(step, c):
        code = heard_s[step, c, me]
        return jnp.where(code < blocks, code, code - blocks), code < blocks

    encoded(target, 0, [dst_s[c, me] for c in range(slots)])

    @pl.loop(1, n)
    def _(step):
        encoded(target, step, [asked(step, c)[0] for c in range(slots)])

    all_near(hand_send, hand_recv).wait()

    for i in own:
        share(1, i).start()
    waited = set()
    for i in passed:
        bit, held = plan[i]
        low = held & -held
        first = plan.index((low, held - low))
        for h in range(2):
            if (h, first) not in waited:
                share(h, first).wait_recv()
                waited.add((h, first))
            share(h, i).start()
    rest = pool.at[pl.ds(0, len(plan) - len(parents))]
    remote(rest, rest, rep_send, rest_recv, to_node(far)).wait_recv()
    sent = pool.at[pl.ds(0, len(plan))]
    remote(sent, sent, rep_send, rest_recv, to_node(far)).wait_send()

    contract = (((1,), (1,)), ((), ()))

    def one_negative(step, o, c):
        pick = picks_s[c, o]
        home = pick // offers
        first = (pick % offers) * per_block
        cand = jnp.concatenate([pool[first + h, home] for h in range(per_block)], axis=0)
        scores = scale * lax.dot_general(
            cand, block(source, step, c), contract, preferred_element_type=jnp.float32
        )
        term = jnp.sum(softplus(scores), axis=0, keepdims=True) * (1.0 / BLK)
        return jnp.where(c < counts_s[0, o], term, 0.0)

    def negatives(step, total):
        o = partner(me, step, n)
        rows = [one_negative(step, o, c) for c in range(slots)]
        out[owners + o] = jnp.concatenate(rows, axis=0)
        return total + functools.reduce(jnp.add, rows)

    total = lax.fori_loop(0, n, negatives, jnp.zeros((1, BLK), jnp.float32))

    diagonal = lax.broadcasted_iota(jnp.int32, (BLK, BLK), 0) == lax.broadcasted_iota(
        jnp.int32, (BLK, BLK), 1
    )

    def positives(held, step, live, total):
        rows = []
        for c in range(slots):
            every = lax.dot_general(
                block(target, step, c), block(held, step, c), contract, preferred_element_type=jnp.float32
            )
            raw = scale * jnp.sum(jnp.where(diagonal, every, 0.0), axis=0, keepdims=True)
            rows.append(jnp.where(live[c], raw, 0.0))
            total = total + jnp.where(live[c], softplus(-raw), 0.0)
        return jnp.concatenate(rows, axis=0), total

    rows, total = positives(source, 0, [c < counts_s[0, me] for c in range(slots)], total)
    out[me] = rows

    def give(step):
        return remote(
            back.at[step], out.at[me], ret_send, ret_recv,
            to_node(source_of(me, step, n)),
        )

    def arrived(step, total):
        send(step).wait_recv()
        rows, total = positives(fetched, step, [asked(step, c)[1] for c in range(slots)], total)
        back[step] = rows
        give(step).start()
        return total

    if n <= UNROLL:
        steps = steps[n // 2 :] + steps[: n // 2]
    total = in_order(steps, arrived, total)

    live_slots = lax.fori_loop(0, owners, lambda o, s: s + counts_s[0, o], jnp.int32(0))
    sums[0, 0:1] = total
    sums[0, 1:2] = jnp.full((1, BLK), live_slots.astype(jnp.float32))

    def tell(dn, dr):
        at = dn * reps + dr
        return remote(
            sums.at[0], sums.at[at], all_send, all_recv,
            {"node": partner(me, dn, n), "rep": partner(rep, dr, reps)},
        )

    @pl.loop(0, n)
    def _(i):
        for dr in reversed(range(reps)):
            if dr:
                tell(n - 1 - i, dr).start()
            else:

                @pl.when(i < n - 1)
                def _():
                    tell(n - 1 - i, 0).start()

    told = sums.at[pl.ds(1, n * reps - 1)]
    for spot, send_sem, recv_sem in (
        (out.at[pl.ds(0, n - 1)], ret_send, ret_recv), (told, all_send, all_recv)
    ):
        remote(spot, spot, send_sem, recv_sem, to_node(far)).wait()
    gone = source.at[pl.ds(1, n - 1)]
    remote(gone, gone, src_send, src_recv.at[0], to_node(far)).wait_send()

    both = jnp.sum(sums[...], axis=0)
    loss = jnp.sum(both[0:1], axis=1, keepdims=True) / (BLK * both[1:2, 0:1])
    out[2 * owners] = jnp.broadcast_to(loss, (slots, BLK))


def split(owners, joined, pos_out, neg_out, loss_out):
    pos_out[...] = joined[0:owners]
    neg_out[...] = joined[owners : 2 * owners]
    loss_out[...] = joined[2 * owners, 0:1, 0:1]


def shards(n, reps, features, w_in, w_out, pos_src, pos_dst, counts, neg_blocks, neg_pick):
    rows, width = features.shape
    owners = pos_dst.shape[2]
    slots = pos_dst.shape[3]
    offers = neg_blocks.shape[1]
    blocks = rows // BLK
    hbm = pl.BlockSpec(memory_space=pltpu.HBM)
    vmem = pl.BlockSpec(memory_space=pltpu.VMEM)
    dma = pltpu.SemaphoreType.DMA
    rows_half = BLK // HALVES
    half = pltpu.VMEM((blocks, rows_half, width), jnp.bfloat16)
    group = pltpu.VMEM((n, HALVES, slots, rows_half, width), jnp.bfloat16)
    parents = len([b for b, held in messages(reps) if b > 1])
    held = features.size + 3 * n * slots * BLK * width + n * offers * BLK * width

    def by_slot(ids):
        return jnp.swapaxes(ids, 2, 3).reshape(slots, owners)

    joined = pl.pallas_call(
        functools.partial(kernel, n, reps, slots, offers),
        out_shape=pltpu.VMEM((2 * owners + 1, slots, BLK), jnp.float32),
        in_specs=[hbm] * 8,
        out_specs=vmem,
        scratch_shapes=[
            half,
            half,
            pltpu.VMEM(w_in.shape, jnp.bfloat16),
            pltpu.VMEM(w_out.shape, jnp.bfloat16),
            pltpu.VMEM((slots, owners), jnp.int32),
            pltpu.VMEM((1, owners), jnp.int32),
            pltpu.VMEM((slots, owners), jnp.int32),
            pltpu.VMEM((n, slots, owners), jnp.int32),
            pltpu.SMEM((3, slots, owners), jnp.int32),
            pltpu.SMEM((1, owners), jnp.int32),
            pltpu.SMEM((1, offers), jnp.int32),
            pltpu.SMEM((n, slots, owners), jnp.int32),
            group,
            group,
            group,
            pltpu.VMEM((n, slots, BLK), jnp.float32),
            pltpu.VMEM((reps, n, offers * BLK // reps, width), jnp.bfloat16),
            pltpu.VMEM((n * reps, 2, BLK), jnp.float32),
            dma((HALVES,)),
            dma((2,)),
            dma((5,)),
            dma,
            dma,
            dma,
            dma,
            dma((n - 1,)),
            dma,
            dma,
            dma,
            dma,
            dma,
            dma,
            dma,
            dma,
            dma,
            dma((max(2 * parents, 1),)),
            dma,
            dma,
            dma,
        ],
        compiler_params=pltpu.CompilerParams(
            collective_id=0, has_side_effects=True, vmem_limit_bytes=2 * held + SPARE
        ),
    )(
        *(
            pltpu.with_memory_space_constraint(array, pltpu.HBM)
            for array in (
                by_slot(pos_src),
                by_slot(pos_dst),
                counts.reshape(1, owners),
                neg_blocks.reshape(1, offers),
                by_slot(neg_pick),
                features.reshape(blocks, HALVES, rows_half, width),
                w_in,
                w_out,
            )
        )
    )
    scores = jax.ShapeDtypeStruct((owners, slots, BLK), jnp.float32)
    pos, neg, loss = pl.pallas_call(
        functools.partial(split, owners),
        out_shape=(scores, scores, jax.ShapeDtypeStruct((1, 1), jnp.float32)),
        in_specs=[vmem],
        out_specs=(vmem, vmem, vmem),
        compiler_params=pltpu.CompilerParams(vmem_limit_bytes=4 * 2**20),
    )(joined)
    shape = (1, 1, owners, slots, BLK)
    return pos.reshape(shape), neg.reshape(shape), loss.reshape(())


def solution(mesh):
    return jax.shard_map(
        functools.partial(shards, mesh.shape["node"], mesh.shape["rep"]),
        mesh=mesh,
        in_specs=(
            P("node", None),
            P(),
            P(),
            P("node", "rep", None, None),
            P("node", "rep", None, None),
            P("node", "rep", None),
            P("node", None),
            P("node", "rep", None, None),
        ),
        out_specs=(P("node", "rep", None, None, None), P("node", "rep", None, None, None), P()),
        check_vma=False,
    )
```

time: 42.4 us -> 38.9 us (0.917)
  Pallas kernels: 41.6 us -> 38.1 us
    pallas_call x1, Pallas kernels: 41 us -> 37.5 us  [shards(): pl.pallas_call(functools.partial(kernel, n, reps, slots, offers), out_sha...]
where the time goes in v2:
time: 38.9 us; the launch traced here: 38.7 us
  Pallas kernels  38.1 us (98%)
  between operations  0.64 us (2%)
    pallas_call x1, Pallas kernels, shards(): pl.pallas_call(functools.partial(kernel, n, reps, slots, offers), out_sha...  37.5 us

profile of v2, /device:TPU:0, one launch (start us, length us, event | category | flops | bytes accessed | tf_op | source)
XLA Modules:
  0.0 38.7 jit_solution(7620211077578226755)
XLA Ops:
  0.6 37.5 %shard_map.103.joined = f32[17,2,128]{2,1,0:T(2,128)S(1)} custom-call(s32[2,8]{1,0:T(2,128)} %bitcast.15, s32[2,8]{1,0:T(2,128)} %bitcast.16, s32[1,8]{1,0:T(1,128)} %bitcast.18, s32[1,2]{1,0:T(1,128)} %neg_ids.1, s32[2,8]{1,0:T(2,128)} %bitcast.17, bf16[160,2,64,256]{3,2,1,0:T(8,128)(2,1)} %bitcast.14, bf16[256,256]{1,0:T(8,128)(2,1)} %w_in.1, ...), custom_call_target="tpu_custom_call" | custom-call | tf_op jit(solution)/shard_map/pallas_call | solution.py:412
  38.1 0.6 %shard_map.104 = (f32[8,2,128]{2,1,0:T(2,128)}, f32[8,2,128]{2,1,0:T(2,128)}, f32[1,1]{1,0:T(1,128)}) custom-call(f32[17,2,128]{2,1,0:T(2,128)S(1)} %shard_map.103.joined), custom_call_target="tpu_custom_call" | custom-call | tf_op jit(solution)/shard_map/pallas_call | solution.py:477

commit v3 on v2

--- a/solution.py
+++ b/solution.py
@@ -8,9 +8,9 @@
 from jax.sharding import PartitionSpec as P
 
 BLK = 128
-HALVES = 2
-EARLY = 2
+EARLY = 4
 UNROLL = 16
+AHEAD = 2
 SPARE = 6 * 2**20
 
 
@@ -45,8 +45,7 @@
     down = list(range(n - 1, 0, -1))
     if n & (n - 1) or n < 4:
         return down
-    far = [n // 2 + 2 * (k % (n // 4)) + k // (n // 4) for k in range(n // 2)]
-    return far + down[n // 2 :]
+    return list(range(n // 2, n)) + down[n // 2 :]
 
 
 def in_order(steps, body, carry):
@@ -67,7 +66,7 @@
     n, reps, slots, offers,
     src_ids, dst_ids, counts, neg_ids, picks, features, w_in, w_out,
     out,
-    feat_a, feat_b, wi_v, wo_v, asks_in, counts_in, asks, heard,
+    feats, wi_v, wo_v, asks_in, counts_in, asks, heard,
     id_s, counts_s, neg_s, heard_s,
     source, target, fetched, back, pool, sums,
     load_sem, weight_sem, id_sem, local_sem,
@@ -77,18 +76,14 @@
 ):
     me = lax.axis_index("node")
     rep = lax.axis_index("rep")
-    blocks, rows, width = feat_a.shape
+    blocks, rows, width = feats[0].shape
     owners = src_ids.shape[1]
     src_s, dst_s, picks_s = (id_s.at[i] for i in range(3))
-    quarter = pool.shape[2]
-    per_block = BLK // quarter
     scale = 1.0 / width**0.5
     part = n // 2
     base = (me // part) * part
     far = (me + part) % n
     steps = sequence(n) if n <= UNROLL else list(range(n - 1, 0, -1))
-    piece_at = (rep % per_block) * quarter
-    first_half = piece_at // rows
 
     def to_node(j):
         return {"node": j}
@@ -100,21 +95,6 @@
         return pltpu.make_async_remote_copy(
             src_ref=src, dst_ref=dst, send_sem=send, recv_sem=recv,
             device_id=where, device_id_type=pl.DeviceIdType.MESH,
-        )
-
-    barrier = pltpu.get_barrier_semaphore()
-
-    @pl.loop(1, n)
-    def _(i):
-        pl.semaphore_signal(
-            barrier, inc=1, device_id=to_node(partner(me, n - i, n)),
-            device_id_type=pl.DeviceIdType.MESH,
-        )
-
-    for step in range(1, reps):
-        pl.semaphore_signal(
-            barrier, inc=1, device_id=to_rep(partner(rep, step, reps)),
-            device_id_type=pl.DeviceIdType.MESH,
         )
 
     weights = [
@@ -132,11 +112,26 @@
     ]
     loads = [
         pltpu.make_async_copy(
-            features.at[pl.ds(0, blocks), (first_half + j) % HALVES], buffer, load_sem.at[j]
-        )
-        for j, buffer in enumerate((feat_a, feat_b))
+            features.at[pl.ds(0, blocks), (rep + j) % reps], buffer, load_sem.at[j]
+        )
+        for j, buffer in enumerate(feats)
     ]
-    for copy in ids + weights + loads:
+    barrier = pltpu.get_barrier_semaphore()
+
+    @pl.loop(1, n)
+    def _(i):
+        pl.semaphore_signal(
+            barrier, inc=1, device_id=to_node(partner(me, n - i, n)),
+            device_id_type=pl.DeviceIdType.MESH,
+        )
+
+    for step in range(1, reps):
+        pl.semaphore_signal(
+            barrier, inc=1, device_id=to_rep(partner(rep, step, reps)),
+            device_id_type=pl.DeviceIdType.MESH,
+        )
+
+    for copy in ids + weights + loads[:AHEAD]:
         copy.start()
     pltpu.make_async_copy(id_s, id_s, id_sem.at[0]).wait()
     for copy in ids[3:]:
@@ -147,15 +142,17 @@
 
     for copy in weights + loads[:1]:
         copy.wait()
+    for copy in loads[AHEAD : AHEAD + 1]:
+        copy.start()
 
     def run(parts):
         return encode(jnp.concatenate(parts, axis=0), wi_v[...], wo_v[...])
 
     def encoded(held, at, ids):
-        both = run([buffer[i] for buffer in (feat_a, feat_b) for i in ids])
-        both = both.reshape(HALVES, slots, rows, width)
-        for j in range(HALVES):
-            held[at, (first_half + j) % HALVES] = both[j]
+        both = run([buffer[i] for buffer in feats for i in ids])
+        both = both.reshape(reps, slots, rows, width)
+        for j in range(reps):
+            held[at, (rep + j) % reps] = both[j]
 
     def source_ids(step):
         o = partner(me, step, n)
@@ -170,19 +167,19 @@
             to_node(partner(me, step, n)),
         )
 
-    def encode_half(step, j, buffer):
-        half = run([buffer[i] for i in source_ids(step)])
-        source[step, (first_half + j) % HALVES] = half.reshape(slots, rows, width)
-
-    def send_half(step, j):
-        h = (first_half + j) % HALVES
+    def encode_part(step, j):
+        part_rows = run([feats[j][i] for i in source_ids(step)])
+        source[step, (rep + j) % reps] = part_rows.reshape(slots, rows, width)
+
+    def send_part(step, j):
+        h = (rep + j) % reps
         return remote(
             source.at[step, h], fetched.at[step, h], src_send, src_recv.at[step - 1],
             to_node(partner(me, step, n)),
         )
 
     def block(held, at, c):
-        return jnp.concatenate([held[at, h, c] for h in range(HALVES)], axis=0)
+        return jnp.concatenate([held[at, h, c] for h in range(reps)], axis=0)
 
     def ask(step):
         return remote(
@@ -199,9 +196,10 @@
         spot = pool.at[rep, pl.ds(0, part - 1)]
         return remote(spot, spot, send_sem, recv_sem, to_node(far))
 
-    piece = pl.ds(pl.multiple_of(piece_at % rows, quarter), quarter)
-    pool[rep, me] = run([feat_a[neg_s[0, rep // per_block], piece]])
-    encode_half(steps[0], 0, feat_a)
+    pool[rep, me] = run([feats[0][neg_s[0, k]] for k in range(offers)]).reshape(
+        offers, rows, width
+    )
+    encode_part(steps[0], 0)
     pl.semaphore_wait(barrier, n - 1 + reps - 1)
 
     across = remote(pool.at[rep, me], pool.at[rep, me], far_send, far_recv, to_node(far))
@@ -215,12 +213,15 @@
     def _(i):
         ask(n - i).start()
 
-    send_half(steps[0], 0).start()
-    loads[1].wait()
-    encode_half(steps[0], 1, feat_b)
+    for j in range(1, reps):
+        loads[j].wait()
+        for copy in loads[j + AHEAD : j + AHEAD + 1]:
+            copy.start()
+        encode_part(steps[0], j)
+        send_part(steps[0], j - 1).start()
     for before, step in zip(steps[:EARLY], steps[1 : EARLY + 1]):
         encode_source(step)
-        (send_half(before, 1) if before == steps[0] else send(before)).start()
+        (send_part(before, reps - 1) if before == steps[0] else send(before)).start()
 
     def prepare(step, carry):
         encode_source(step)
@@ -299,8 +300,8 @@
     def one_negative(step, o, c):
         pick = picks_s[c, o]
         home = pick // offers
-        first = (pick % offers) * per_block
-        cand = jnp.concatenate([pool[first + h, home] for h in range(per_block)], axis=0)
+        offer = pick % offers
+        cand = jnp.concatenate([pool[r, home, offer] for r in range(reps)], axis=0)
         scores = scale * lax.dot_general(
             cand, block(source, step, c), contract, preferred_element_type=jnp.float32
         )
@@ -400,9 +401,8 @@
     hbm = pl.BlockSpec(memory_space=pltpu.HBM)
     vmem = pl.BlockSpec(memory_space=pltpu.VMEM)
     dma = pltpu.SemaphoreType.DMA
-    rows_half = BLK // HALVES
-    half = pltpu.VMEM((blocks, rows_half, width), jnp.bfloat16)
-    group = pltpu.VMEM((n, HALVES, slots, rows_half, width), jnp.bfloat16)
+    part = BLK // reps
+    group = pltpu.VMEM((n, reps, slots, part, width), jnp.bfloat16)
     parents = len([b for b, held in messages(reps) if b > 1])
     held = features.size + 3 * n * slots * BLK * width + n * offers * BLK * width
 
@@ -415,8 +415,7 @@
         in_specs=[hbm] * 8,
         out_specs=vmem,
         scratch_shapes=[
-            half,
-            half,
+            [pltpu.VMEM((blocks, part, width), jnp.bfloat16)] * reps,
             pltpu.VMEM(w_in.shape, jnp.bfloat16),
             pltpu.VMEM(w_out.shape, jnp.bfloat16),
             pltpu.VMEM((slots, owners), jnp.int32),
@@ -431,9 +430,9 @@
             group,
             group,
             pltpu.VMEM((n, slots, BLK), jnp.float32),
-            pltpu.VMEM((reps, n, offers * BLK // reps, width), jnp.bfloat16),
+            pltpu.VMEM((reps, n, offers, part, width), jnp.bfloat16),
             pltpu.VMEM((n * reps, 2, BLK), jnp.float32),
-            dma((HALVES,)),
+            dma((reps,)),
             dma((2,)),
             dma((5,)),
             dma,
@@ -467,7 +466,7 @@
                 counts.reshape(1, owners),
                 neg_blocks.reshape(1, offers),
                 by_slot(neg_pick),
-                features.reshape(blocks, HALVES, rows_half, width),
+                features.reshape(blocks, reps, part, width),
                 w_in,
                 w_out,
             )

time: 38.9 us -> 38.4 us (0.987)
  Pallas kernels: 38.1 us -> 37.6 us
    pallas_call x1, Pallas kernels: 37.5 us -> 37 us  [shards(): pl.pallas_call(functools.partial(kernel, n, reps, slots, offers), out_sha...]
where the time goes in v3:
time: 38.4 us; the launch traced here: 38.3 us
  Pallas kernels  37.6 us (98%)
  between operations  0.64 us (2%)
    pallas_call x1, Pallas kernels, shards(): pl.pallas_call(functools.partial(kernel, n, reps, slots, offers), out_sha...  37 us

profile of v3, /device:TPU:0, one launch (start us, length us, event | category | flops | bytes accessed | tf_op | source)
XLA Modules:
  0.0 38.3 jit_solution(7111611006722211845)
XLA Ops:
  0.6 37.0 %shard_map.103.joined = f32[17,2,128]{2,1,0:T(2,128)S(1)} custom-call(s32[2,8]{1,0:T(2,128)} %bitcast.15, s32[2,8]{1,0:T(2,128)} %bitcast.16, s32[1,8]{1,0:T(1,128)} %bitcast.18, s32[1,2]{1,0:T(1,128)} %neg_ids.1, s32[2,8]{1,0:T(2,128)} %bitcast.17, bf16[160,4,32,256]{3,2,1,0:T(8,128)(2,1)} %bitcast.14, bf16[256,256]{1,0:T(8,128)(2,1)} %w_in.1, ...), custom_call_target="tpu_custom_call" | custom-call | tf_op jit(solution)/shard_map/pallas_call | solution.py:412
  37.7 0.6 %shard_map.104 = (f32[8,2,128]{2,1,0:T(2,128)}, f32[8,2,128]{2,1,0:T(2,128)}, f32[1,1]{1,0:T(1,128)}) custom-call(f32[17,2,128]{2,1,0:T(2,128)S(1)} %shard_map.103.joined), custom_call_target="tpu_custom_call" | custom-call | tf_op jit(solution)/shard_map/pallas_call | solution.py:476

commit v4 on v3

--- a/solution.py
+++ b/solution.py
@@ -83,6 +83,7 @@
     part = n // 2
     base = (me // part) * part
     far = (me + part) % n
+    early = min(EARLY, n - 2)
     steps = sequence(n) if n <= UNROLL else list(range(n - 1, 0, -1))
 
     def to_node(j):
@@ -112,7 +113,7 @@
     ]
     loads = [
         pltpu.make_async_copy(
-            features.at[pl.ds(0, blocks), (rep + j) % reps], buffer, load_sem.at[j]
+            features.at[pl.ds(0, blocks), (rep + j) % reps], buffer, load_sem.at[j % AHEAD]
         )
         for j, buffer in enumerate(feats)
     ]
@@ -219,7 +220,7 @@
             copy.start()
         encode_part(steps[0], j)
         send_part(steps[0], j - 1).start()
-    for before, step in zip(steps[:EARLY], steps[1 : EARLY + 1]):
+    for before, step in zip(steps[:early], steps[1 : early + 1]):
         encode_source(step)
         (send_part(before, reps - 1) if before == steps[0] else send(before)).start()
 
@@ -227,7 +228,7 @@
         encode_source(step)
         return carry
 
-    in_order(steps[EARLY + 1 :], prepare, 0)
+    in_order(steps[early + 1 :], prepare, 0)
     encode_source(0)
 
     across.wait()
@@ -257,7 +258,7 @@
         send(step).start()
         return carry
 
-    in_order(steps[EARLY:], release, 0)
+    in_order(steps[early:], release, 0)
 
     got = heard.at[pl.ds(1, n - 1)]
     remote(got, got, ask_send, ask_recv, to_node(far)).wait()
@@ -432,7 +433,7 @@
             pltpu.VMEM((n, slots, BLK), jnp.float32),
             pltpu.VMEM((reps, n, offers, part, width), jnp.bfloat16),
             pltpu.VMEM((n * reps, 2, BLK), jnp.float32),
-            dma((reps,)),
+            dma((AHEAD,)),
             dma((2,)),
             dma((5,)),
             dma,

time: 38.4 us -> 38.4 us (level)
  no operation moved by 1% of the time
where the time goes in v4:
time: 38.4 us; the launch traced here: 38.3 us
  Pallas kernels  37.6 us (98%)
  between operations  0.64 us (2%)
    pallas_call x1, Pallas kernels, shards(): pl.pallas_call(functools.partial(kernel, n, reps, slots, offers), out_sha...  37 us

profile of v4, /device:TPU:0, one launch (start us, length us, event | category | flops | bytes accessed | tf_op | source)
XLA Modules:
  0.0 38.3 jit_solution(6197781822768922709)
XLA Ops:
  0.6 37.0 %shard_map.103.joined = f32[17,2,128]{2,1,0:T(2,128)S(1)} custom-call(s32[2,8]{1,0:T(2,128)} %bitcast.15, s32[2,8]{1,0:T(2,128)} %bitcast.16, s32[1,8]{1,0:T(1,128)} %bitcast.18, s32[1,2]{1,0:T(1,128)} %neg_ids.1, s32[2,8]{1,0:T(2,128)} %bitcast.17, bf16[160,4,32,256]{3,2,1,0:T(8,128)(2,1)} %bitcast.14, bf16[256,256]{1,0:T(8,128)(2,1)} %w_in.1, ...), custom_call_target="tpu_custom_call" | custom-call | tf_op jit(solution)/shard_map/pallas_call | solution.py:413
  37.7 0.6 %shard_map.104 = (f32[8,2,128]{2,1,0:T(2,128)}, f32[8,2,128]{2,1,0:T(2,128)}, f32[1,1]{1,0:T(1,128)}) custom-call(f32[17,2,128]{2,1,0:T(2,128)S(1)} %shard_map.103.joined), custom_call_target="tpu_custom_call" | custom-call | tf_op jit(solution)/shard_map/pallas_call | solution.py:477
